TPU v7x, 32 devices: a whole 2x2x4 slice. The times are simulated.
32 devices in a mesh: dp: 8 (over y, x, core), tensor: 4 (over z).
Axes of the slice: x: 2, y: 2, z: 4, core: 2. Of those that a mesh axis runs over, the one named last changes fastest.
Arguments:
- hidden_in: bfloat16 [16384, 1024], P(('dp', 'tensor')), may hold values from -6 to 6
- cotangent: bfloat16 [16384, 1024], P(('dp', 'tensor')), may hold values from -6 to 6
- w_query: float32 [1024, 1024], P('dp', 'tensor'), may hold values from -0.1875 to 0.1875
- w_key: float32 [1024, 1024], P('dp', 'tensor'), may hold values from -0.1875 to 0.1875
- w_value: float32 [1024, 1024], P('dp', 'tensor'), may hold values from -0.1875 to 0.1875
- w_out: float32 [1024, 1024], P('dp', 'tensor'), may hold values from -2 to 2
- w_up: float32 [1024, 4096], P('dp', 'tensor'), may hold values from -0.1875 to 0.1875
- w_down: float32 [1024, 4096], P('dp', 'tensor'), may hold values from -0.09375 to 0.09375
- bias_query: float32 [1024], replicated, may hold values from -3 to 3
- bias_value: float32 [1024], replicated, may hold values from -3 to 3
- bias_out: float32 [1024], replicated, may hold values from -3 to 3
- bias_up: float32 [4096], replicated, may hold values from -3 to 3
- bias_down: float32 [1024], replicated, may hold values from -3 to 3
- gain_attn: float32 [1024], replicated, may hold values from 0.5 to 1.5
- shift_attn: float32 [1024], replicated, may hold values from -3 to 3
- gain_ffn: float32 [1024], replicated, may hold values from 0.5 to 1.5
- shift_ffn: float32 [1024], replicated, may hold values from -3 to 3
- valid_lengths: int32 [32], P('dp'), may hold values from 64 to 512, as said below
Outputs:
- output: bfloat16 [16384, 1024], P(('dp', 'tensor'))
- grad_hidden_in: bfloat16 [16384, 1024], P(('dp', 'tensor'))
- grad_w_query: float32 [1024, 1024], P('dp', 'tensor')
- grad_w_key: float32 [1024, 1024], P('dp', 'tensor')
- grad_w_value: float32 [1024, 1024], P('dp', 'tensor')
- grad_w_out: float32 [1024, 1024], P('dp', 'tensor')
- grad_w_up: float32 [1024, 4096], P('dp', 'tensor')
- grad_w_down: float32 [1024, 4096], P('dp', 'tensor')
- grad_bias_query: float32 [1024], replicated
- grad_bias_value: float32 [1024], replicated
- grad_bias_out: float32 [1024], replicated
- grad_bias_up: float32 [4096], replicated
- grad_bias_down: float32 [1024], replicated
- grad_gain_attn: float32 [1024], replicated
- grad_shift_attn: float32 [1024], replicated
- grad_gain_ffn: float32 [1024], replicated
- grad_shift_ffn: float32 [1024], replicated
Inputs may be any that keep to these rules, and one draw needn't show every extreme that they name: Each sequence's real tokens are its first valid_lengths positions; some sequence has all 512.
All inputs are finite; a program needn't handle non-finite values.
Results may differ from a plain program's by a relative error of at most 0.02.
Values may be sent and summed in bfloat16 or wider, within the bound.
A program may use at most 128 MiB of HBM per device.

v0:
```python
import math

import jax
import jax.numpy as jnp
from jax import lax
from jax.experimental import pallas as pl
from jax.experimental.pallas import tpu as pltpu
from jax.sharding import PartitionSpec as P

HEADS = 16
EPSILON = 1e-12
MASKED = -1e30
BF16 = jnp.bfloat16
F32 = jnp.float32

ORDER = (0, 2, 4, 6, 1, 3, 5, 7)
BIT_CORE, BIT_X, BIT_Y = 1, 2, 4


def matmul(left_side, right_side):
    return jnp.dot(left_side, right_side, preferred_element_type=F32)


def contract_rows(left_side, right_side):
    return lax.dot_general(
        left_side, right_side, (((0,), (0,)), ((), ())), preferred_element_type=F32
    )


def contract_cols(left_side, right_side):
    return lax.dot_general(
        left_side, right_side, (((1,), (1,)), ((), ())), preferred_element_type=F32
    )


FORWARD_ID = 1
BACKWARD_ID = 2
TILE = 512

FORWARD = (
    "lplane9", "z1", "z3", "lcor9", "col1", "z2", "z5", "z0", "z4", "col3", "col2", "prep",
    "col5", "col0", "cor2", "cor1", "z6", "cor0", "cor3", "z7", "last0", "z8", "col4", "col6",
    "last2", "tr", "last1", "cor5", "cor4", "qkv", "last3", "lz9", "a0", "cor6", "a1", "a2",
    "col7", "a3", "last4", "last5", "last6", "out", "col8", "norm", "up1", "cor7", "cor8",
    "lcore9", "up2", "up3", "last7", "lowX", "last8", "low1", "low2", "ln",
)
BACKWARD = (
    "oth8", "oth7", "gelA", "own8", "cor8", "own7", "cor7", "oth9", "oth4", "sid8", "gelB",
    "own9", "sid7", "oth5", "lz9", "oth6", "upA", "own4", "upB", "own5", "cor4", "cor5", "norm",
    "col8", "sid4", "own6", "out", "col7", "oth3", "a0", "own3", "cor3", "cor6", "a1", "col4",
    "sid5", "sid3", "a2", "a3", "oth1", "sid6", "vec", "oth2", "col5", "fin4", "own1", "cor1",
    "v0", "oth0", "col3", "v1", "own2", "cor2", "fin8", "sid1", "col6", "own0", "cor0", "fin7",
    "sid2", "v2", "col1", "dxA", "sid0", "col2", "lcor9", "dxB", "fin6", "col0", "v3", "sid9",
    "fin2", "v4", "gout", "fin5", "fin1", "fin3", "fin9", "v5", "fin0",
)


def neighbour(index, bit):
    return index + bit - 2 * bit * ((index // bit) % 2)


def block_of(index, mask):
    for bit in (BIT_CORE, BIT_X, BIT_Y):
        if mask & bit:
            index = neighbour(index, bit)
    return index


def pieces_of(size, attn, units_each):
    pieces = [(0, k * size * attn, attn) for k in range(3)] + [(1, 0, attn)]
    for weight in (2, 3):
        start = 0
        for count in (units_each // 2, units_each // 4, units_each // 4):
            pieces.append((weight, start * size, count))
            start += count
    return pieces


def run_events(order, table, attend, size):
    first = order.index("a0")
    last = order.index(f"a{size - 1}")
    for name in order[:first]:
        table[name]()

    def step(r, carry):
        attend(r)
        for k in range(size - 1):
            start = order.index(f"a{k}") + 1
            names = order[start : order.index(f"a{k + 1}")]
            if names:

                @pl.when(r == k)
                def _():
                    for name in names:
                        table[name]()

        return carry

    lax.fori_loop(0, size, step, 0)
    for name in order[last + 1 :]:
        table[name]()


def greet(partners):
    barrier = pltpu.get_barrier_semaphore()
    for partner in partners:
        pl.semaphore_signal(
            barrier, inc=1, device_id=partner, device_id_type=pl.DeviceIdType.MESH
        )
    pl.semaphore_wait(barrier, len(partners))


def forward_near(weights, hidden_in, cotangent, wide, bias_query, bias_value, bias_units, lengths, head_size):
    size = lax.axis_size("tensor")
    rows, width = hidden_in.shape
    block = width // len(ORDER)
    attn, units_each = weights[0].shape[1], weights[4].shape[1]
    cols = [3 * attn, attn, units_each, units_each]
    full = [(width, size * c) for c in cols]
    units = size * units_each
    half = block // 2
    pieces = pieces_of(size, attn, units_each)
    X = len(pieces) - 1
    A, O, U, _ = range(4)
    B_OUT, B_DOWN, G_ATTN, S_ATTN, G_FFN, S_FFN = range(6)

    def body(
        q_in, k_in, v_in, o_in, u_in, d_in, hidden_raw, cotangent_ref, bias_out_in, bias_down_in,
        gain_attn_in, shift_attn_in, gain_ffn_in, shift_ffn_in, bias_q_ref, bias_v_ref, bias_u_ref,
        lengths_ref,
        a_out, o_out, u_out, d_out, qkv_out, context_out, hidden_out, active_out, slope_out, output_ref,
        mixed_ref, mixed_t, normed_t, input_t, second_ref, sums_ref, wide_ref,
        a_ref, o_ref, u_ref, d_ref, x_ref, low_ref, active_ref, slope_ref, bias_ref, units_ref, qkv_ref,
        context_ref, hidden_ref, turned_x, turned_n, local_sem, send_sem, recv_sem,
        tile_sem,
    ):
        data_at, tensor_at = lax.axis_index("dp"), lax.axis_index("tensor")
        places = (a_ref, o_ref, u_ref, d_ref)

        def dp_partner(bit):
            return (neighbour(data_at, bit), tensor_at)

        def z_partner(step):
            return by_z[step]

        by_z = [(data_at, (tensor_at + step) % size) for step in range(size)]
        by_x, by_y, by_core = dp_partner(BIT_X), dp_partner(BIT_Y), dp_partner(BIT_CORE)
        owners = [block_of(data_at, mask) for mask in ORDER]
        copies = {}

        def send(g, slot, source, target, device):
            def copy():
                return pltpu.make_async_remote_copy(
                    src_ref=source,
                    dst_ref=target,
                    send_sem=send_sem.at[g, slot],
                    recv_sem=recv_sem.at[g, slot],
                    device_id=device,
                    device_id_type=pl.DeviceIdType.MESH,
                )

            copies[g, slot] = copy
            copy().start()

        def arrived(g, *slots):
            for slot in slots:
                copies[g, slot]().wait_recv()

        def whole(g, start, count):
            weight, first, wide_by = pieces[g]
            return places[weight].at[start : start + count, first : first + size * wide_by]

        def cell(g, start, count, r):
            weight, first, wide_by = pieces[g]
            at = first + r * wide_by
            return places[weight].at[start : start + count, at : at + wide_by]

        def send_z(g):
            for r in range(1, size):
                send(g, r - 1, cell(g, 0, block, 0), cell(g, 0, block, r), z_partner(r))

        def send_column(g):
            arrived(g, 0, 1, 2)
            send(g, 3, whole(g, 0, block), whole(g, block, block), by_x)
            send(g, 4, whole(g, 0, block), whole(g, 2 * block, block), by_y)

        def send_corner(g):
            arrived(g, 3, 4)
            send(g, 5, whole(g, block, half), whole(g, 3 * block, half), by_y)
            send(g, 6, whole(g, 2 * block + half, half), whole(g, 3 * block + half, half), by_x)
            send(g, 7, whole(g, 0, 3 * block), whole(g, 4 * block, 3 * block), by_core)

        def send_last(g):
            arrived(g, 5, 6)
            send(g, 8, whole(g, 3 * block, block), whole(g, 7 * block, block), by_core)

        def complete(*group):
            for g in group:
                arrived(g, 7, 8)

        def late_plane():
            send(X, 3, cell(X, 0, block, 0), cell(X, block, block, 0), by_x)
            send(X, 4, cell(X, 0, block, 0), cell(X, 2 * block, block, 0), by_y)

        def late_corner():
            arrived(X, 3, 4)
            send(X, 5, cell(X, block, half, 0), cell(X, 3 * block, half, 0), by_y)
            send(X, 6, cell(X, 2 * block + half, half, 0), cell(X, 3 * block + half, half, 0), by_x)

        def late_z():
            arrived(X, 5, 6)
            for r in range(1, size):
                send(X, r - 1, cell(X, 0, 4 * block, 0), cell(X, 0, 4 * block, r), z_partner(r))

        def late_core():
            arrived(X, 0, 1, 2)
            send(X, 7, whole(X, 0, 4 * block), whole(X, 4 * block, 4 * block), by_core)

        saves = []

        def save(slot, source, target):
            copy = pltpu.make_async_copy(source, target, local_sem.at[slot])
            copy.start()
            saves.append(copy)

        def save_weight(slot, g):
            target = (a_out, o_out, u_out, d_out)[g]
            save(slot, places[g], target)

        sources = (q_in, k_in, v_in, o_in, u_in, u_in, u_in, d_in, d_in, d_in)

        def cast(g):
            weight, first, wide_by = pieces[g]
            start = first // size if weight >= U else 0
            places[weight][:block, first : first + wide_by] = sources[g][
                :, start : start + wide_by
            ].astype(BF16)

        for g in range(len(pieces)):
            cast(g)
        greet([by_x, by_y, by_core] + by_z[1:])

        def lanes_of(owner):
            return pl.ds(pl.multiple_of(owner * block, block), block)

        def turn(target, at, rows_of):
            for k in range(width // 128):
                target[k * 128 : (k + 1) * 128, at] = rows_of[:, k * 128 : (k + 1) * 128].T.astype(BF16)

        def vector(k):
            return wide_ref[k : k + 1, :]

        def column_of(r, first, span):
            at = ((tensor_at + size - r) % size) * (first[1]) + first[0]
            return pl.ds(pl.multiple_of(at, 128), span)

        def prepare():
            for place, owner in enumerate(owners):
                at = slice(place * block, (place + 1) * block)
                x_ref[:, at] = hidden_raw[:, lanes_of(owner)]
                for k, ref in enumerate(
                    (bias_out_in, bias_down_in, gain_attn_in, shift_attn_in, gain_ffn_in, shift_ffn_in)
                ):
                    wide_ref[k : k + 1, at] = ref[:, lanes_of(owner)]
            for r in range(size):
                at = slice(r * attn, (r + 1) * attn)
                bias_ref[0:1, at] = bias_q_ref[:, column_of(r, (0, attn), attn)]
                bias_ref[1:2, at] = bias_v_ref[:, column_of(r, (0, attn), attn)]
                for weight, first, wide_by in pieces:
                    if weight == U:
                        at = slice(first + r * wide_by, first + (r + 1) * wide_by)
                        units_ref[:, at] = bias_u_ref[
                            :, column_of(r, (first // size, units_each), wide_by)
                        ]

        def turn_inputs():
            def one(j, carry):
                at = pl.ds(pl.multiple_of(j * 128, 128), 128)
                turn(turned_x, at, x_ref[at, :].astype(F32))
                return carry

            lax.fori_loop(0, rows // 128, one, 0)
            save(4, turned_x, input_t)

        def project(j, carry):
            at = pl.ds(pl.multiple_of(j * attn, attn), attn)
            total = matmul(x_ref[...], a_ref[:, at])
            which = j // size
            bias = bias_ref[:, pl.ds(pl.multiple_of((j % size) * attn, attn), attn)]
            bias = jnp.where(which == 0, bias[0:1], jnp.where(which == 2, bias[1:2], 0.0))
            qkv_ref[:, at] = (total + bias).astype(BF16)
            return carry

        def qkv():
            complete(0, 1, 2)
            save_weight(A, A)
            lax.fori_loop(0, 3 * size, project, 0)
            save(5, qkv_ref, qkv_out)

        scale = float(head_size) ** (-0.5)
        length = lengths_ref[tensor_at]

        def attend(r):
            seen = lax.broadcasted_iota(jnp.int32, (rows, rows), 1) < length
            for start, lanes, held in pairs_of(attn, head_size):
                at = [
                    pl.ds(pl.multiple_of((k * size + r) * attn + start, 128), lanes) for k in range(3)
                ]
                queries, keys, values = (qkv_ref[:, where] for where in at)
                total = jnp.zeros((rows, lanes), F32)
                for which in range(held):
                    probs = soft_weights(keep_head(queries, which, head_size), keys, seen, scale)
                    total += keep_head(matmul(probs.astype(BF16), values), which, head_size)
                context_ref[:, at[0]] = total.astype(BF16)

        def output(j, carry):
            at = pl.ds(pl.multiple_of(j * 256, 256), 256)
            total = contract_cols(context_ref[...], o_ref[at, :])
            hidden_ref[:, at] = x_ref[:, at].astype(F32) + total + wide_ref[B_OUT : B_OUT + 1, at]
            return carry

        def out():
            complete(3)
            save_weight(O, O)
            save(6, context_ref, context_out)
            lax.fori_loop(0, width // 256, output, 0)
            save(7, hidden_ref, hidden_out)

        chunk = 128

        def norm_step(j, carry):
            at = pl.ds(pl.multiple_of(j * chunk, chunk), chunk)
            normed = norm_forward(hidden_ref[at, :], vector(G_ATTN), vector(S_ATTN))[0]
            low_ref[at, :] = normed.astype(BF16)
            second_ref[at, :] = normed + vector(B_DOWN)
            turn(turned_n, at, normed)
            return carry

        def norm():
            lax.fori_loop(0, rows // chunk, norm_step, 0)
            save(8, turned_n, normed_t)

        def tile_at(j):
            return pl.ds(pl.multiple_of(j * TILE, TILE), TILE)

        def slope_copy(j):
            return pltpu.make_async_copy(
                slope_ref.at[j % 2], slope_out.at[:, tile_at(j)], tile_sem.at[1, j % 2]
            )

        def active_copy(j):
            return pltpu.make_async_copy(
                active_ref.at[:, tile_at(j)], active_out.at[:, tile_at(j)], tile_sem.at[0, j]
            )

        def raise_up(j, carry):
            @pl.when(j >= 2)
            def _():
                slope_copy(j - 2).wait()

            total = matmul(low_ref[...], u_ref[:, tile_at(j)])
            active, slope = activate(total, units_ref[:, tile_at(j)])
            active_ref[:, tile_at(j)] = active.astype(BF16)
            slope_ref[j % 2] = slope
            active_copy(j).start()
            slope_copy(j).start()
            return carry

        def span_of(g):
            _, first, wide_by = pieces[g]
            return slice(first, first + size * wide_by)

        def raise_piece(g):
            complete(g)
            save(g + 5, u_ref.at[:, span_of(g)], u_out.at[:, span_of(g)])
            at = span_of(g)
            lax.fori_loop(at.start // TILE, at.stop // TILE, raise_up, 0)

        def lower_piece(g):
            if g == X:
                arrived(X, 7)
            else:
                complete(g)
            at = span_of(g)
            save(g + 5, d_ref.at[:, at], d_out.at[:, at])

            def one(j, carry):
                to = pl.ds(pl.multiple_of(j * 256, 256), 256)
                second_ref[:, to] += contract_cols(active_ref[:, at], d_ref[to, at])
                return carry

            lax.fori_loop(0, width // 256, one, 0)

        def second(j, sums):
            at = pl.ds(pl.multiple_of(j * chunk, chunk), chunk)
            result, normal, root = norm_forward(second_ref[at, :], vector(G_FFN), vector(S_FFN))
            grads = jnp.concatenate([cotangent_ref[at, lanes_of(owner)] for owner in owners], axis=1)
            for place, owner in enumerate(owners):
                output_ref[at, lanes_of(owner)] = result[:, place * block : (place + 1) * block].astype(BF16)
            hidden, more_gain, more_shift = norm_backward(
                grads.astype(F32), normal, root, vector(G_FFN)
            )
            second_ref[at, :] = hidden
            mixed_ref[at, :] = hidden.astype(BF16)
            turn(mixed_t, at, hidden)
            more = (jnp.sum(hidden, axis=0), more_gain, more_shift)
            return tuple(a + b[None] for a, b in zip(sums, more))

        def last_norm():
            zero = jnp.zeros((1, width), F32)
            sums = lax.fori_loop(0, rows // chunk, second, (zero, zero, zero))
            for k in range(3):
                sums_ref[k : k + 1, :] = sums[k]

        def bound(step, *given):
            return lambda: step(*given)

        table = {
            "prep": prepare, "tr": turn_inputs, "qkv": qkv, "out": out, "norm": norm, "ln": last_norm,
            "up1": bound(raise_piece, 4), "up2": bound(raise_piece, 5), "up3": bound(raise_piece, 6),
            "low1": bound(lower_piece, 7), "low2": bound(lower_piece, 8), "lowX": bound(lower_piece, X),
            "lplane9": late_plane, "lcor9": late_corner, "lz9": late_z, "lcore9": late_core,
        }
        for g in range(X):
            table[f"z{g}"] = bound(send_z, g)
            table[f"col{g}"] = bound(send_column, g)
            table[f"cor{g}"] = bound(send_corner, g)
            table[f"last{g}"] = bound(send_last, g)
        run_events(FORWARD, table, attend, size)

        def settle(j, carry):
            active_copy(j).wait()
            return carry

        lax.fori_loop(0, units // TILE, settle, 0)
        for j in (units // TILE - 2, units // TILE - 1):
            slope_copy(j).wait()
        for copy in saves:
            copy.wait()
        for copy in copies.values():
            copy().wait_send()

    anywhere, inside = pl.BlockSpec(memory_space=pl.ANY), pl.BlockSpec(memory_space=pltpu.VMEM)
    tall = jax.ShapeDtypeStruct((rows, width), BF16)
    turned = jax.ShapeDtypeStruct((width, rows), BF16)
    return pl.pallas_call(
        body,
        out_shape=[jax.ShapeDtypeStruct(shape, BF16) for shape in full]
        + [
            jax.ShapeDtypeStruct((rows, full[A][1]), BF16),
            tall,
            jax.ShapeDtypeStruct((rows, width), F32),
            jax.ShapeDtypeStruct((rows, units), BF16),
            jax.ShapeDtypeStruct((rows, units), F32),
            tall,
            tall,
            turned,
            turned,
            turned,
            jax.ShapeDtypeStruct((rows, width), F32),
            jax.ShapeDtypeStruct((3, width), F32),
            jax.ShapeDtypeStruct((6, width), F32),
        ],
        in_specs=[inside] * 17 + [pl.BlockSpec(memory_space=pltpu.SMEM)],
        out_specs=[anywhere] * 9 + [inside] * 3 + [anywhere] * 2 + [inside] * 3,
        scratch_shapes=[pltpu.VMEM(shape, BF16) for shape in full]
        + [
            pltpu.VMEM((rows, width), BF16),
            pltpu.VMEM((rows, width), BF16),
            pltpu.VMEM((rows, units), BF16),
            pltpu.VMEM((2, rows, TILE), F32),
            pltpu.VMEM((2, size * attn), F32),
            pltpu.VMEM((1, units), F32),
            pltpu.VMEM((rows, full[A][1]), BF16),
            pltpu.VMEM((rows, width), BF16),
            pltpu.VMEM((rows, width), F32),
            pltpu.VMEM((width, rows), BF16),
            pltpu.VMEM((width, rows), BF16),
            pltpu.SemaphoreType.DMA((5 + len(pieces),)),
            pltpu.SemaphoreType.DMA((len(pieces), 9)),
            pltpu.SemaphoreType.DMA((len(pieces), 9)),
            pltpu.SemaphoreType.DMA((2, units // TILE)),
        ],
        compiler_params=pltpu.CompilerParams(
            collective_id=FORWARD_ID, has_side_effects=True, vmem_limit_bytes=63 * 2**20
        ),
        cost_estimate=pl.CostEstimate(
            flops=2 * rows * width * sum(shape[1] for shape in full),
            bytes_accessed=4 * width * sum(shape[1] for shape in full),
            transcendentals=rows * units,
        ),
        name="forward_near",
    )(
        *weights, hidden_in, cotangent, *(vector[None] for vector in wide), bias_query[None],
        bias_value[None], bias_units[None], lengths,
    )


def backward_near(mixed_low, mixed_t, normed_t, input_t, context, grad_second, hidden, wide, lengths,
                  active, slope, qkv, weights, vectors, head_size):
    size = lax.axis_size("tensor")
    rows, width = mixed_low.shape
    block = width // len(ORDER)
    middle = width // 2
    half = block // 2
    full = [weight.shape[1] for weight in weights]
    units = full[2]
    units_each = units // size
    attn = full[1] // size
    pieces = pieces_of(size, attn, units_each)
    X = len(pieces) - 1
    A, O, U, D = range(4)
    tiles = [c // TILE for c in full]
    vector_rows = (6 * width + 2 * full[1] + units) // 128
    v_query, v_value, v_up = 6 * width // 128, (6 * width + full[1]) // 128, (6 * width + 2 * full[1]) // 128
    scale = float(head_size) ** (-0.5)

    def body(
        mixed_in, mixed_t, normed_in, input_in, context_in, second_in, hidden_in, wide_ref,
        lengths_ref, active_in, slope_in, qkv_in, a_in, o_in, u_in, d_in, vectors_ref,
        q_out, k_out, v_out, o_out, u_out, d_out, grad_out, sums_out,
        w_buf, act_ref, slope_buf, gu_ref, grad_ref, low_ref, low_t, gctx_ref, qkv_buf, send_buf,
        units_sum, mixed_ref, normed_t, input_t, context_ref, a_plane, o_plane, u_plane, d_plane, *rest,
    ):
        count = len(pieces)
        corners, sides, zins = (rest[k * count : (k + 1) * count] for k in range(3))
        (
            v_ref, v_in, load_sem, start_sem, core_send, core_recv, send_sem, recv_sem, v_send, v_recv,
        ) = rest[3 * count :]
        data_at, tensor_at = lax.axis_index("dp"), lax.axis_index("tensor")
        planes = (a_plane, o_plane, u_plane, d_plane)
        outs = (q_out, k_out, v_out, o_out, u_out, u_out, u_out, d_out, d_out, d_out)
        shift_by = (tiles[O], 0, 0, 0)

        def dp_partner(bit):
            return (neighbour(data_at, bit), tensor_at)

        def z_partner(step):
            return by_z[step % size]

        by_z = [(data_at, (tensor_at + step) % size) for step in range(size)]

        by_x, by_y, by_core = dp_partner(BIT_X), dp_partner(BIT_Y), dp_partner(BIT_CORE)

        def column(j, span=TILE):
            return pl.ds(pl.multiple_of(j * span, 128), span)

        def load(row, source, buffer, j):
            return pltpu.make_async_copy(
                source.at[:, column(j)], buffer.at[j % 2], load_sem.at[row, j % 2]
            )

        def over_tiles(first, last, loads, step):
            for row, source, buffer in loads:
                load(row, source, buffer, first).start()

            def one(j, carry):
                @pl.when(j + 1 < last)
                def _():
                    for row, source, buffer in loads:
                        load(row, source, buffer, j + 1).start()

                for row, source, buffer in loads:
                    load(row, source, buffer, j).wait()
                step(j)
                return carry

            lax.fori_loop(first, last, one, 0)

        def remote(source, target, send, receive, device):
            return pltpu.make_async_remote_copy(
                src_ref=source,
                dst_ref=target,
                send_sem=send,
                recv_sem=receive,
                device_id=device,
                device_id_type=pl.DeviceIdType.MESH,
            )

        def core_copy(g, j):
            return remote(
                send_buf.at[:, column(j + shift_by[g])],
                planes[g].at[:, column(j)],
                core_send.at[g, j],
                core_recv.at[g, j],
                by_core,
            )

        copies = {}

        def send(g, slot, source, target, device):
            def copy():
                return remote(source, target(), send_sem.at[g, slot], recv_sem.at[g, slot], device)

            copies[g, slot] = copy
            copy().start()

        def arrived(g, *slots):
            for slot in slots:
                copies[g, slot]().wait_recv()

        def other_tile(g, left_t, right, j):
            send_buf[:, column(j + shift_by[g])] = matmul(left_t[middle:, :], right).astype(BF16)
            core_copy(g, j).start()

        def own_tile(g, left_t, right, j):
            core_copy(g, j).wait_recv()
            total = matmul(left_t[:middle, :], right) + planes[g][:, column(j)].astype(F32)
            planes[g][:, column(j)] = total.astype(BF16)

        def span(g):
            _, first, wide_by = pieces[g]
            return first, wide_by if g == X else size * wide_by

        def plane_rows(g, start, count):
            first, wide_by = span(g)
            return planes[pieces[g][0]].at[start : start + count, first : first + wide_by]

        def send_corner(g):
            send(g, 0, plane_rows(g, 3 * block, half), lambda: corners[g].at[0], by_x)
            send(g, 1, plane_rows(g, 3 * block + half, half), lambda: corners[g].at[1], by_y)

        def add_rows(g, start, count, *more):
            plane = planes[pieces[g][0]]
            first, wide_by = span(g)
            step = min(TILE, wide_by)
            for at in range(0, wide_by, step):
                where = (slice(start, start + count), slice(first + at, first + at + step))
                total = plane[where].astype(F32)
                for ref in more:
                    total += ref[:, at : at + step].astype(F32)
                plane[where] = total.astype(BF16)

        def send_sides(g):
            arrived(g, 0, 1)
            add_rows(g, 2 * block, half, corners[g].at[0])
            add_rows(g, block + half, half, corners[g].at[1])
            send(g, 2, plane_rows(g, block, block), lambda: sides[g].at[0], by_x)
            send(g, 3, plane_rows(g, 2 * block, block), lambda: sides[g].at[1], by_y)

        def out_of(g):
            weight, first, wide_by = pieces[g]
            start = first // size if weight >= U else 0
            return outs[g].at[:, start : start + wide_by]

        def send_column(g):
            arrived(g, 2, 3)
            weight, first, wide_by = pieces[g]
            for r in range(size):
                at = slice(r * wide_by, (r + 1) * wide_by)
                own = slice(first + r * wide_by, first + (r + 1) * wide_by)
                total = planes[weight][:block, own].astype(F32)
                total += sides[g][0, :, at].astype(F32) + sides[g][1, :, at].astype(F32)
                if r == 0:
                    out_of(g)[...] = total
                else:
                    planes[weight][:block, own] = total.astype(BF16)
                    send(g, 3 + r, planes[weight].at[:block, own], lambda r=r: zins[g].at[r - 1], z_partner(-r))

        def finish(g):
            arrived(g, *range(4, 3 + size))
            total = out_of(g)[...]
            for r in range(1, size):
                total += zins[g][r - 1].astype(F32)
            out_of(g)[...] = total

        def late_z():
            weight, first, wide_by = pieces[X]
            for r in range(1, size):
                own = slice(first + r * wide_by, first + (r + 1) * wide_by)
                send(X, 3 + r, planes[weight].at[:, own], lambda r=r: zins[X].at[r - 1], z_partner(-r))

        def late_corner():
            arrived(X, *range(4, 3 + size))
            for k in range(4):
                rows_k = slice(k * block, (k + 1) * block)
                add_rows(X, k * block, block, *(zins[X].at[r, rows_k] for r in range(size - 1)))
            send_corner(X)

        def late_finish():
            arrived(X, 2, 3)
            total = plane_rows(X, 0, block)[...].astype(F32)
            out_of(X)[...] = total + sides[X][0].astype(F32) + sides[X][1].astype(F32)

        def feature_rows(k, vector):
            for place, mask in enumerate(ORDER):
                at = block_of(data_at, mask)
                v_ref[0, pl.ds(k * len(ORDER) + at, 1), :] = vector[:, place * 128 : (place + 1) * 128]

        z_near = tensor_at + 1 - 2 * (tensor_at % 2)
        z_across = tensor_at + 2 - 4 * ((tensor_at // 2) % 2)
        v_partners = (by_core, (data_at, z_near), (data_at, z_across), by_x, by_y)

        def v_copy(k):
            return remote(v_ref.at[k], v_in.at[k], v_send.at[k], v_recv.at[k], v_partners[k])

        def v_add(k):
            v_copy(k).wait_recv()
            v_ref[k + 1] = v_ref[k] + v_in[k]

        early = [
            pltpu.make_async_copy(
                active_in.at[:, k * (units // 2) : (k + 1) * (units // 2)],
                act_ref.at[:, k * (units // 2) : (k + 1) * (units // 2)],
                start_sem.at[k],
            )
            for k in range(2)
        ]
        grad_load, mixed_load, normed_load, context_load, input_load = (
            pltpu.make_async_copy(source, target, start_sem.at[k])
            for k, (source, target) in enumerate(
                (
                    (second_in, grad_ref),
                    (mixed_in, mixed_ref),
                    (normed_in, normed_t),
                    (context_in, context_ref),
                    (input_in, input_t),
                ),
                2,
            )
        )
        for copy in early:
            copy.start()
        for copy in (mixed_load, normed_load, grad_load, context_load, input_load):
            copy.start()
        greet([by_x, by_y, by_core] + by_z[1:])

        def each(first, last, step):
            def one(j, carry):
                step(j)
                return carry

            lax.fori_loop(first, last, one, 0)

        def other_down(j):
            other_tile(D, mixed_t, act_ref[:, column(j)], j)

        def own_down(j):
            own_tile(D, mixed_t, act_ref[:, column(j)], j)

        def other_up(j):
            core_copy(D, j).wait_send()
            other_tile(U, normed_t, gu_ref[:, column(j)], j)

        def own_up(j):
            own_tile(U, normed_t, gu_ref[:, column(j)], j)

        def bounds(g):
            _, first, wide_by = pieces[g]
            return first // TILE, (first + size * wide_by) // TILE

        early[0].wait()
        early[1].wait()

        def loaded(copy, step):
            def both():
                copy.wait()
                step()

            return both

        def bound(step, *given):
            return lambda: step(*given)

        def gelu_step(j):
            low = (matmul(mixed_ref[...], w_buf[j % 2]) * slope_buf[j % 2]).astype(BF16)
            gu_ref[:, column(j)] = low
            units_sum[:, column(j)] = jnp.sum(low.astype(F32), axis=0, keepdims=True)

        gelu_loads = [(1, d_in, w_buf), (2, slope_in, slope_buf)]
        hidden_loads = [
            pltpu.make_async_copy(hidden_in.at[:, column(k)], slope_buf.at[k], load_sem.at[2, k])
            for k in range(2)
        ]

        def second_gelu():
            over_tiles(tiles[D] // 2, tiles[D], gelu_loads, gelu_step)
            for copy in hidden_loads:
                copy.start()

        def up_step(j):
            grad_ref[...] += contract_cols(gu_ref[:, column(j)], w_buf[j % 2])

        def sum_units():
            for k in range(3):
                feature_rows((1, 4, 5)[k], vectors_ref[k : k + 1, :])
            for r in range(size):
                for weight, first, wide_by in pieces:
                    if weight == U:
                        for k in range(wide_by // 128):
                            place = ((tensor_at + size - r) % size) * (units_each // 128)
                            place += (first // size) // 128 + k
                            at = first + r * wide_by + k * 128
                            v_ref[0, pl.ds(v_up + place, 1), :] = units_sum[:, at : at + 128]

        chunk = 128

        def norm_step(j, sums):
            at = pl.ds(pl.multiple_of(j * chunk, chunk), chunk)
            hidden_rows = jnp.concatenate([slope_buf[0, at, :], slope_buf[1, at, :]], axis=1)
            gain = wide_ref[2:3, :]
            normal, root = norm_forward(hidden_rows, gain, gain)[1:]
            hidden, more_gain, more_shift = norm_backward(grad_ref[at, :], normal, root, gain)
            grad_ref[at, :] = hidden
            low_ref[at, :] = hidden.astype(BF16)
            for k in range(width // 128):
                low_t[k * 128 : (k + 1) * 128, at] = hidden[:, k * 128 : (k + 1) * 128].T.astype(BF16)
            more = (jnp.sum(hidden, axis=0), more_gain, more_shift)
            return tuple(a + b[None] for a, b in zip(sums, more))

        def norm():
            for copy in hidden_loads:
                copy.wait()
            zero = jnp.zeros((1, width), F32)
            sums = lax.fori_loop(0, rows // chunk, norm_step, (zero, zero, zero))
            for k in range(3):
                feature_rows((0, 2, 3)[k], sums[k])

        def out_step(j):
            core_copy(U, j).wait_send()
            gctx_ref[:, column(j)] = matmul(low_ref[...], w_buf[j % 2]).astype(BF16)
            other_tile(O, low_t, context_ref[:, column(j)], j)

        def out():
            context_load.wait()
            over_tiles(0, tiles[O], [(1, o_in, w_buf)], out_step)
            for copy in qkv_load(0):
                copy.start()

        def own_out():
            for j in range(tiles[O]):
                own_tile(O, low_t, context_ref[:, j * TILE : (j + 1) * TILE], j)

        def qkv_load(r):
            return [
                pltpu.make_async_copy(
                    qkv_in.at[:, column(k * size + r, attn)], qkv_buf.at[r % 2, k], load_sem.at[k, r % 2]
                )
                for k in range(3)
            ]

        def attend_step(r):
            @pl.when(r + 1 < size)
            def _():
                for copy in qkv_load(r + 1):
                    copy.start()

            for copy in qkv_load(r):
                copy.wait()
            slot = r % 2
            seen = lax.broadcasted_iota(jnp.int32, (rows, rows), 0) < length
            for start, lanes, held in pairs_of(attn, head_size):
                queries, keys, values = (qkv_buf[slot, k, :, start : start + lanes] for k in range(3))
                grads = gctx_ref[:, pl.ds(pl.multiple_of(r * attn + start, 128), lanes)]
                grad_q = jnp.zeros((rows, lanes), F32)
                grad_k = jnp.zeros((rows, lanes), F32)
                grad_v = jnp.zeros((rows, lanes), F32)
                for which in range(held):
                    mine = keep_head(grads, which, head_size)
                    query = keep_head(queries, which, head_size)
                    scores = jnp.where(seen, contract_cols(keys, query) * scale, MASKED)
                    exponent = jnp.exp(scores - jnp.max(scores, axis=0, keepdims=True))
                    probs = exponent * (1.0 / jnp.sum(exponent, axis=0, keepdims=True))
                    grad_v += matmul(probs.astype(BF16), mine)
                    grad_probs = contract_cols(values, mine)
                    inner = jnp.sum(probs * grad_probs, axis=0, keepdims=True)
                    grad_scores = (probs * (grad_probs - inner)).astype(BF16)
                    grad_q += keep_head(contract_rows(grad_scores, keys), which, head_size)
                    grad_k += matmul(grad_scores, query)
                low_q = (grad_q * scale).astype(BF16)
                low_v = grad_v.astype(BF16)
                for k, low in enumerate((low_q, (grad_k * scale).astype(BF16), low_v)):
                    at = pl.multiple_of((k * size + r) * attn + start, 128)
                    gu_ref[:, pl.ds(at, lanes)] = low
                place = ((tensor_at + size - r) % size) * (attn // 128) + start // 128
                v_ref[0, pl.ds(v_query + place, 1), :] = jnp.sum(
                    low_q.astype(F32), axis=0, keepdims=True
                )
                v_ref[0, pl.ds(v_value + place, 1), :] = jnp.sum(
                    low_v.astype(F32), axis=0, keepdims=True
                )

        length = lengths_ref[tensor_at]

        def other_qkv(j):
            core_copy(U, j + tiles[O]).wait_send()
            other_tile(A, input_t, gu_ref[:, column(j)], j)

        def own_qkv(j):
            own_tile(A, input_t, gu_ref[:, column(j)], j)

        def input_step(j):
            grad_ref[...] += contract_cols(gu_ref[:, column(j)], w_buf[j % 2])

        def give_input():
            for place, mask in enumerate(ORDER):
                at = block_of(data_at, mask)
                grad_out[:, pl.ds(pl.multiple_of(at * block, block), block)] = grad_ref[
                    :, place * block : (place + 1) * block
                ].astype(BF16)

        def give_sums():
            v_add(4)
            sums_out[...] = v_ref[5]

        def next_sum(k):
            v_add(k - 1)
            v_copy(k).start()

        weight_loads = [[(1, ref, w_buf)] for ref in (a_in, o_in, u_in, d_in)]
        parts = (
            (other_qkv, own_qkv), (other_qkv, own_qkv), (other_qkv, own_qkv), (lambda j: None, own_out),
            (other_up, own_up), (other_up, own_up), (other_up, own_up), (other_down, own_down),
            (other_down, own_down), (other_down, own_down),
        )
        halves = [(0, count // 2, count) for count in tiles]
        table = {
            "gelA": loaded(mixed_load, bound(over_tiles, 0, halves[D][1], gelu_loads, gelu_step)),
            "gelB": second_gelu,
            "upA": loaded(grad_load, bound(over_tiles, 0, halves[U][1], weight_loads[U], up_step)),
            "upB": bound(over_tiles, *halves[U][1:], weight_loads[U], up_step),
            "vec": sum_units,
            "norm": norm,
            "out": out,
            "dxA": bound(over_tiles, 0, halves[A][1], weight_loads[A], input_step),
            "dxB": bound(over_tiles, *halves[A][1:], weight_loads[A], input_step),
            "gout": give_input,
            "lz9": late_z,
            "lcor9": late_corner,
            "sid9": bound(send_sides, X),
            "fin9": late_finish,
            "v0": lambda: v_copy(0).start(),
            "v5": give_sums,
        }
        for k in range(1, 5):
            table[f"v{k}"] = bound(next_sum, k)
        for g in range(len(pieces)):
            other, own = parts[g]
            table[f"oth{g}"] = bound(each, *bounds(g), other)
            table[f"own{g}"] = bound(each, *bounds(g), own)
            if g < X:
                table[f"cor{g}"] = bound(send_corner, g)
                table[f"sid{g}"] = bound(send_sides, g)
                table[f"col{g}"] = bound(send_column, g)
                table[f"fin{g}"] = bound(finish, g)
        table["oth3"] = lambda: None
        table["own3"] = own_out
        first_up = [g for g in range(len(pieces)) if f"oth{g}" in BACKWARD and pieces[g][0] == U]
        first_up = min(first_up, key=lambda g: BACKWARD.index(f"oth{g}"))
        table[f"oth{first_up}"] = loaded(normed_load, table[f"oth{first_up}"])
        first_in = min((0, 1, 2), key=lambda g: BACKWARD.index(f"oth{g}"))
        table[f"oth{first_in}"] = loaded(input_load, table[f"oth{first_in}"])
        run_events(BACKWARD, table, attend_step, size)
        for g in (A, O):
            for j in range(tiles[g]):
                core_copy(g, j).wait_send()
        for k in range(5):
            v_copy(k).wait_send()
        for copy in copies.values():
            copy().wait_send()

    spans = [piece[2] if g == X else size * piece[2] for g, piece in enumerate(pieces)]
    anywhere, inside = pl.BlockSpec(memory_space=pl.ANY), pl.BlockSpec(memory_space=pltpu.VMEM)
    results = pl.pallas_call(
        body,
        out_shape=[jax.ShapeDtypeStruct((block, attn), F32)] * 4
        + [jax.ShapeDtypeStruct((block, units_each), F32)] * 2
        + [
            jax.ShapeDtypeStruct((rows, width), BF16),
            jax.ShapeDtypeStruct((vector_rows, 128), F32),
        ],
        in_specs=[anywhere, inside]
        + [anywhere] * 5
        + [inside, pl.BlockSpec(memory_space=pltpu.SMEM)]
        + [anywhere] * 7
        + [inside],
        out_specs=[inside] * 8,
        scratch_shapes=[
            pltpu.VMEM((2, width, TILE), BF16),
            pltpu.VMEM((rows, units), BF16),
            pltpu.VMEM((2, rows, TILE), F32),
            pltpu.VMEM((rows, units), BF16),
            pltpu.VMEM((rows, width), F32),
            pltpu.VMEM((rows, width), BF16),
            pltpu.VMEM((width, rows), BF16),
            pltpu.VMEM((rows, full[1]), BF16),
            pltpu.VMEM((2, 3, rows, attn), BF16),
            pltpu.VMEM((middle, units), BF16),
            pltpu.VMEM((1, units), F32),
            pltpu.VMEM((rows, width), BF16),
            pltpu.VMEM((width, rows), BF16),
            pltpu.VMEM((width, rows), BF16),
            pltpu.VMEM((rows, width), BF16),
        ]
        + [pltpu.VMEM((middle, c), BF16) for c in full]
        + [pltpu.VMEM((2, half, c), BF16) for c in spans]
        + [pltpu.VMEM((2, block, c), BF16) for c in spans]
        + [
            pltpu.VMEM((size - 1, 4 * block if g == X else block, piece[2]), BF16)
            for g, piece in enumerate(pieces)
        ]
        + [
            pltpu.VMEM((6, vector_rows, 128), F32),
            pltpu.VMEM((5, vector_rows, 128), F32),
            pltpu.SemaphoreType.DMA((3, 2)),
            pltpu.SemaphoreType.DMA((7,)),
            pltpu.SemaphoreType.DMA((4, units // TILE)),
            pltpu.SemaphoreType.DMA((4, units // TILE)),
            pltpu.SemaphoreType.DMA((len(pieces), 3 + size)),
            pltpu.SemaphoreType.DMA((len(pieces), 3 + size)),
            pltpu.SemaphoreType.DMA((5,)),
            pltpu.SemaphoreType.DMA((5,)),
        ],
        compiler_params=pltpu.CompilerParams(
            collective_id=BACKWARD_ID, has_side_effects=True, vmem_limit_bytes=63 * 2**20
        ),
        cost_estimate=pl.CostEstimate(
            flops=4 * rows * sum(full) * width,
            bytes_accessed=4 * sum(full) * width,
            transcendentals=0,
        ),
        name="backward_near",
    )(
        mixed_low, mixed_t, normed_t, input_t, context, grad_second, hidden, wide, lengths, active,
        slope, qkv, *weights, vectors,
    )
    return results[:6], results[6], results[7]


def gather_far(shard):
    return lax.all_gather(
        lax.all_gather(shard, "tensor", axis=1, tiled=True), "dp", axis=0, tiled=True
    )


def scatter_far(left_side, right_side):
    whole = contract_rows(left_side, right_side).astype(BF16)
    part = lax.psum_scatter(whole, "dp", scatter_dimension=0, tiled=True)
    return lax.psum_scatter(part, "tensor", scatter_dimension=1, tiled=True).astype(F32)


def soft_weights(queries, keys, visible, scale):
    scores = contract_cols(queries, keys) * scale
    scores = jnp.where(visible, scores, MASKED)
    exponent = jnp.exp(scores - jnp.max(scores, axis=-1, keepdims=True))
    return exponent * (1.0 / jnp.sum(exponent, axis=-1, keepdims=True))


def pairs_of(width, head_size):
    lanes = max(128, head_size)
    return [(start, lanes, lanes // head_size) for start in range(0, width, lanes)]


def keep_head(array, which, head_size):
    lane = lax.broadcasted_iota(jnp.int32, array.shape, 1)
    return jnp.where(lane // head_size == which, array, jnp.zeros_like(array))


def attend_forward(qkv_q, qkv_kv, length, head_size, groups):
    q_rows = qkv_q.shape[0]
    k_rows = qkv_kv.shape[0]
    block = qkv_q.shape[1] // groups
    width = block // 3
    scale = float(head_size) ** (-0.5)

    def body(length_ref, q_ref, kv_ref, out_ref):
        visible = lax.broadcasted_iota(jnp.int32, (q_rows, k_rows), 1) < length_ref[0]
        for start, lanes, held in pairs_of(width, head_size):
            queries = q_ref[:, start : start + lanes]
            keys = kv_ref[:, width + start : width + start + lanes]
            values = kv_ref[:, 2 * width + start : 2 * width + start + lanes]
            total = jnp.zeros((q_rows, lanes), F32)
            for which in range(held):
                probs = soft_weights(keep_head(queries, which, head_size), keys, visible, scale)
                total += keep_head(matmul(probs.astype(BF16), values), which, head_size)
            out_ref[:, start : start + lanes] = total.astype(BF16)

    return pl.pallas_call(
        body,
        out_shape=jax.ShapeDtypeStruct((q_rows, groups * width), BF16),
        grid_spec=pltpu.PrefetchScalarGridSpec(
            num_scalar_prefetch=1,
            grid=(groups,),
            in_specs=[
                pl.BlockSpec((q_rows, block), lambda g, length_ref: (0, g)),
                pl.BlockSpec((k_rows, block), lambda g, length_ref: (0, g)),
            ],
            out_specs=pl.BlockSpec((q_rows, width), lambda g, length_ref: (0, g)),
        ),
        cost_estimate=pl.CostEstimate(
            flops=4 * q_rows * k_rows * width * groups,
            bytes_accessed=2 * (2 * q_rows + 2 * k_rows) * width * groups,
            transcendentals=q_rows * k_rows * groups * width // head_size,
        ),
        name="attend_forward",
    )(length, qkv_q, qkv_kv)


def attend_backward(qkv_q, qkv_kv, grad_context, length, head_size, groups):
    q_rows = qkv_q.shape[0]
    k_rows = qkv_kv.shape[0]
    block = qkv_q.shape[1] // groups
    width = block // 3
    scale = float(head_size) ** (-0.5)

    def body(length_ref, q_ref, kv_ref, grad_ref, dq_ref, dkv_ref):
        visible = lax.broadcasted_iota(jnp.int32, (q_rows, k_rows), 1) < length_ref[0]
        for start, lanes, held in pairs_of(width, head_size):
            queries = q_ref[:, start : start + lanes]
            keys = kv_ref[:, width + start : width + start + lanes]
            values = kv_ref[:, 2 * width + start : 2 * width + start + lanes]
            grads = grad_ref[:, start : start + lanes]
            grad_q = jnp.zeros((q_rows, lanes), F32)
            grad_k = jnp.zeros((k_rows, lanes), F32)
            grad_v = jnp.zeros((k_rows, lanes), F32)
            for which in range(held):
                mine = keep_head(grads, which, head_size)
                query = keep_head(queries, which, head_size)
                probs = soft_weights(query, keys, visible, scale)
                grad_v += contract_rows(probs.astype(BF16), mine)
                grad_probs = contract_cols(mine, values)
                inner = jnp.sum(probs * grad_probs, axis=-1, keepdims=True)
                grad_scores = (probs * (grad_probs - inner)).astype(BF16)
                grad_q += keep_head(matmul(grad_scores, keys), which, head_size)
                grad_k += contract_rows(grad_scores, query)
            dq_ref[:, start : start + lanes] = (grad_q * scale).astype(BF16)
            dkv_ref[:, start : start + lanes] = (grad_k * scale).astype(BF16)
            dkv_ref[:, width + start : width + start + lanes] = grad_v.astype(BF16)

    return pl.pallas_call(
        body,
        out_shape=(
            jax.ShapeDtypeStruct((q_rows, groups * width), BF16),
            jax.ShapeDtypeStruct((k_rows, groups * 2 * width), BF16),
        ),
        grid_spec=pltpu.PrefetchScalarGridSpec(
            num_scalar_prefetch=1,
            grid=(groups,),
            in_specs=[
                pl.BlockSpec((q_rows, block), lambda g, length_ref: (0, g)),
                pl.BlockSpec((k_rows, block), lambda g, length_ref: (0, g)),
                pl.BlockSpec((q_rows, width), lambda g, length_ref: (0, g)),
            ],
            out_specs=[
                pl.BlockSpec((q_rows, width), lambda g, length_ref: (0, g)),
                pl.BlockSpec((k_rows, 2 * width), lambda g, length_ref: (0, g)),
            ],
        ),
        cost_estimate=pl.CostEstimate(
            flops=10 * q_rows * k_rows * width * groups,
            bytes_accessed=2 * (3 * q_rows + 4 * k_rows) * width * groups,
            transcendentals=q_rows * k_rows * groups * width // head_size,
        ),
        name="attend_backward",
    )(length, qkv_q, qkv_kv, grad_context)


def activate(total, bias):
    upper = total + bias
    cumulative = 0.5 * (1.0 + lax.erf(upper * math.sqrt(0.5)))
    density = jnp.exp(-0.5 * upper * upper) * (1.0 / math.sqrt(2.0 * math.pi))
    return upper * cumulative, cumulative + upper * density


def norm_forward(hidden, gain_vec, shift_vec):
    center = hidden - jnp.mean(hidden, axis=-1, keepdims=True)
    variance = jnp.mean(center * center, axis=-1, keepdims=True)
    inv_root = lax.rsqrt(variance + EPSILON)
    normal = center * inv_root
    return (normal * gain_vec + shift_vec, normal, inv_root)


def norm_backward(grad_in, normal, inv_root, gain_vec):
    grad_normal = grad_in * gain_vec
    grad_gain = jnp.sum(grad_in * normal, axis=0)
    grad_shift = jnp.sum(grad_in, axis=0)
    grad_hidden = inv_root * (
        grad_normal
        - jnp.mean(grad_normal, axis=-1, keepdims=True)
        - normal * jnp.mean(grad_normal * normal, axis=-1, keepdims=True)
    )
    return (grad_hidden, grad_gain, grad_shift)


def layer(
    hidden_in,
    cotangent,
    w_query,
    w_key,
    w_value,
    w_out,
    w_up,
    w_down,
    bias_query,
    bias_value,
    bias_out,
    bias_up,
    bias_down,
    gain_attn,
    shift_attn,
    gain_ffn,
    shift_ffn,
    valid_lengths,
):
    rows, model_width = hidden_in.shape
    n_tensor = lax.axis_size("tensor")
    n_data = lax.axis_size("dp")
    tensor_at = lax.axis_index("tensor")
    spread_over = rows * n_tensor // valid_lengths.shape[0] // rows
    head_size = model_width // HEADS
    head_cols = w_query.shape[1]
    factor = 1.0 / math.sqrt(rows * n_tensor * n_data)
    matrices = (w_query, w_key, w_value, w_out, w_up, w_down)
    wide = (bias_out, bias_down, gain_attn, shift_attn, gain_ffn, shift_ffn)

    if n_data == len(ORDER) and spread_over == 1:
        (
            qkv_full, out_full, up_full, down_full, qkv, context, hidden, active, slope, output,
            mixed_low, mixed_t, normed_t, input_t, grad_second, given, arranged,
        ) = forward_near(
            matrices, hidden_in, cotangent, wide, bias_query, bias_value, bias_up, valid_lengths,
            head_size,
        )
        grads, grad_input, sums = backward_near(
            mixed_low, mixed_t, normed_t, input_t, context, grad_second, hidden, arranged,
            valid_lengths, active, slope, qkv, (qkv_full, out_full, up_full, down_full), given,
            head_size,
        )
        sums = sums.reshape(-1) * factor
    else:

        def column_part(vector):
            return vector.reshape(n_tensor, -1)

        query_bias, value_bias = column_part(bias_query), column_part(bias_value)
        bias_qkv = jnp.concatenate(
            [query_bias, jnp.zeros_like(query_bias), value_bias], axis=1
        ).reshape(1, -1)
        length = lax.dynamic_slice_in_dim(valid_lengths, tensor_at // spread_over, 1)
        low = [matrix.astype(BF16) for matrix in matrices]
        shards = [jnp.concatenate(low[:3], axis=1)] + low[3:]
        qkv_full, out_full, up_full, down_full = (gather_far(shard) for shard in shards)
        qkv = (matmul(hidden_in, qkv_full) + bias_qkv).astype(BF16)
        members = [list(range(k, k + spread_over)) for k in range(0, n_tensor, spread_over)]
        qkv_seq = lax.all_gather(qkv, "tensor", axis_index_groups=members, axis=0, tiled=True)
        context = attend_forward(qkv, qkv_seq, length, head_size, n_tensor)
        hidden = hidden_in.astype(F32) + contract_cols(context, out_full) + bias_out
        normed, normal_attn, root_attn = norm_forward(hidden, gain_attn, shift_attn)
        normed_low = normed.astype(BF16)
        active, slope = activate(matmul(normed_low, up_full), bias_up)
        active = active.astype(BF16)
        mixed = contract_cols(active, down_full)
        result, normal_ffn, root_ffn = norm_forward(normed + mixed + bias_down, gain_ffn, shift_ffn)
        output = result.astype(BF16)
        grad_second, grad_gain_ffn, grad_shift_ffn = norm_backward(
            cotangent.astype(F32), normal_ffn, root_ffn, gain_ffn
        )
        grad_bias_down = jnp.sum(grad_second, axis=0)
        mixed_low = grad_second.astype(BF16)
        grad_down = scatter_far(mixed_low, active)
        grad_upper = (matmul(mixed_low, down_full) * slope).astype(BF16)
        grad_bias_up = jnp.sum(grad_upper, axis=0, dtype=F32)
        grad_up = scatter_far(normed_low, grad_upper)
        grad_normed = grad_second + contract_cols(grad_upper, up_full)
        grad_first, grad_gain_attn, grad_shift_attn = norm_backward(
            grad_normed, normal_attn, root_attn, gain_attn
        )
        grad_bias_out = jnp.sum(grad_first, axis=0)
        attn_low = grad_first.astype(BF16)
        grad_context = matmul(attn_low, out_full).astype(BF16)
        grad_out = scatter_far(attn_low, context)
        grad_q, grad_kv = attend_backward(qkv, qkv_seq, grad_context, length, head_size, n_tensor)
        grad_kv = lax.psum_scatter(
            grad_kv.astype(F32),
            "tensor",
            scatter_dimension=0,
            axis_index_groups=members,
            tiled=True,
        ).astype(BF16)
        grad_qkv = jnp.concatenate(
            [grad_q.reshape(rows, n_tensor, -1), grad_kv.reshape(rows, n_tensor, -1)], axis=2
        ).reshape(rows, -1)
        grad_bias_qkv = jnp.sum(grad_qkv, axis=0, dtype=F32).reshape(n_tensor, 3, head_cols)
        grads = jnp.split(scatter_far(hidden_in, grad_qkv), 3, axis=1)
        grads += [grad_out, grad_up, grad_down]
        grad_input = (grad_first + contract_cols(grad_qkv, qkv_full)).astype(BF16)
        sums = jnp.concatenate(
            [
                grad_bias_out,
                grad_bias_down,
                grad_gain_attn,
                grad_shift_attn,
                grad_gain_ffn,
                grad_shift_ffn,
                grad_bias_qkv[:, 0].reshape(-1),
                grad_bias_qkv[:, 2].reshape(-1),
                grad_bias_up,
            ]
        )
        sums = lax.psum(sums, ("dp", "tensor")) * factor
    v_out, v_down, v_gain_attn, v_shift_attn, v_gain_ffn, v_shift_ffn, v_query, v_value = (
        sums[k * model_width : (k + 1) * model_width] for k in range(8)
    )
    v_up = sums[8 * model_width :]
    return (
        output,
        grad_input,
        *(grad * factor for grad in grads),
        v_query,
        v_value,
        v_out,
        v_up,
        v_down,
        v_gain_attn,
        v_shift_attn,
        v_gain_ffn,
        v_shift_ffn,
    )


def solution(mesh):
    tokens, matrix, copied = P(("dp", "tensor"), None), P("dp", "tensor"), P()
    return jax.shard_map(
        layer,
        mesh=mesh,
        in_specs=(tokens,) * 2 + (matrix,) * 6 + (copied,) * 9 + (P("dp"),),
        out_specs=(tokens,) * 2 + (matrix,) * 6 + (copied,) * 9,
        check_vma=False,
    )
```

profile of v0, /device:TPU:0, one launch (start us, length us, event | category | flops | bytes accessed | tf_op | source)
XLA Modules:
  0.0 260.7 jit_solution(17874560444822489450)
XLA Ops:
  0.7 127.3 %forward_near.1 = (bf16[1024,3072]{1,0:T(8,128)(2,1)}, bf16[1024,1024]{1,0:T(8,128)(2,1)}, bf16[1024,4096]{1,0:T(8,128)(2,1)}, bf16[1024,4096]{1,0:T(8,128)(2,1)...) custom-call(f32[128,256]{1,0:T(8,128)} %q_in.1, ...), custom_call_target="tpu_custom_call" | custom-call | flops 12884901888 | bytes 50331648 | tf_op jit(solution)/shard_map/forward_near/pallas_call | solution.py:446
  128.0 121.7 %backward_near.1 = (f32[128,256]{1,0:T(8,128)}, f32[128,256]{1,0:T(8,128)}, f32[128,256]{1,0:T(8,128)}, f32[128,256]{1,0:T(8,128)}, f32[128,1024]{1,0:T(8,128)},...) custom-call(bf16[512,1024]{1,0:T(8,128)(2,1)} %get-tuple-element.43.mixed_in, ...), custom_call_target="tpu_custom_call" | custom-call | flops 25769803776 | bytes 50331648 | tf_op jit(solution)/shard_map/backward_near/pallas_call | solution.py:964
  249.7 0.0 copy-start
  249.7 0.9 broadcast_multiply_fusion.6
  250.6 0.6 slice_bitcast_fusion
  251.2 0.6 slice_bitcast_fusion.1
  251.9 1.7 broadcast_multiply_fusion.4
  253.5 1.7 broadcast_multiply_fusion.2
  255.2 2.3 broadcast_multiply_fusion
  257.5 2.3 copy.37
  259.8 0.0 copy-done
  259.8 1.0 copy.38
Async XLA Ops:
  249.7 10.0 %copy-start = (bf16[512,1024]{1,0:T(8,128)(2,1)S(1)}, bf16[512,1024]{1,0:T(8,128)(2,1)}, u32[]{:S(2)}) copy-start(bf16[512,1024]{1,0:T(8,128)(2,1)} %get-tuple-element.99) | copy-start | bytes 3145732
where the time goes:
time: 261 us
  Pallas kernels  249 us (95%)
  other arithmetic  6.54 us (3%)
  local copies, waits for them, and re-layouts  4.47 us (2%)
    pallas_call x1, Pallas kernels, forward_near(): pl.pallas_call(body, out_shape=[jax.ShapeDtypeStruct(shape, BF16) for sha...  127 us
    pallas_call x1, Pallas kernels, backward_near(): pl.pallas_call(body, out_shape=[jax.ShapeDtypeStruct((block, attn), F32)]...  122 us
    mul x3, other arithmetic, layer(): grad * factor  5.65 us

commit v1 on v0

--- a/solution.py
+++ b/solution.py
@@ -107,7 +107,30 @@
         pl.semaphore_signal(
             barrier, inc=1, device_id=partner, device_id_type=pl.DeviceIdType.MESH
         )
-    pl.semaphore_wait(barrier, len(partners))
+
+
+def await_greetings(partners):
+    pl.semaphore_wait(pltpu.get_barrier_semaphore(), len(partners))
+
+
+def scale_and_copy(scaled, copied, sums, lengths, factor):
+    arrays = list(scaled) + list(copied)
+    starts = [sum(lengths[:k]) for k in range(len(lengths))]
+
+    def body(*refs):
+        sums_ref, targets = refs[len(arrays)], refs[len(arrays) + 1 :]
+        for k in range(len(arrays)):
+            targets[k][...] = refs[k][...] * factor if k < len(scaled) else refs[k][...]
+        for start, length, target in zip(starts, lengths, targets[len(arrays) :]):
+            target[...] = sums_ref[start : start + length, :] * factor
+
+    return pl.pallas_call(
+        body,
+        out_shape=[jax.ShapeDtypeStruct(array.shape, array.dtype) for array in arrays]
+        + [jax.ShapeDtypeStruct((length, sums.shape[1]), F32) for length in lengths],
+        in_specs=[pl.BlockSpec(memory_space=pltpu.VMEM)] * (len(arrays) + 1),
+        out_specs=[pl.BlockSpec(memory_space=pltpu.VMEM)] * (len(arrays) + len(lengths)),
+    )(*arrays, sums)
 
 
 def forward_near(weights, hidden_in, cotangent, wide, bias_query, bias_value, bias_units, lengths, head_size):
@@ -236,9 +259,11 @@
                 :, start : start + wide_by
             ].astype(BF16)
 
+        partners = [by_x, by_y, by_core] + by_z[1:]
+        greet(partners)
         for g in range(len(pieces)):
             cast(g)
-        greet([by_x, by_y, by_core] + by_z[1:])
+        await_greetings(partners)
 
         def lanes_of(owner):
             return pl.ds(pl.multiple_of(owner * block, block), block)
@@ -723,7 +748,9 @@
             copy.start()
         for copy in (mixed_load, normed_load, grad_load, context_load, input_load):
             copy.start()
-        greet([by_x, by_y, by_core] + by_z[1:])
+        partners = [by_x, by_y, by_core] + by_z[1:]
+        greet(partners)
+        await_greetings(partners)
 
         def each(first, last, step):
             def one(j, carry):
@@ -1226,7 +1253,10 @@
             valid_lengths, active, slope, qkv, (qkv_full, out_full, up_full, down_full), given,
             head_size,
         )
-        sums = sums.reshape(-1) * factor
+        lengths = [model_width // 128] * 8 + [bias_up.shape[0] // 128]
+        results = scale_and_copy(grads, (grad_input, output), sums, lengths, factor)
+        grads, (grad_input, output) = results[:6], results[6:8]
+        vector_sums = [part.reshape(-1) for part in results[8:]]
     else:
 
         def column_part(vector):
@@ -1282,7 +1312,7 @@
         ).reshape(rows, -1)
         grad_bias_qkv = jnp.sum(grad_qkv, axis=0, dtype=F32).reshape(n_tensor, 3, head_cols)
         grads = jnp.split(scatter_far(hidden_in, grad_qkv), 3, axis=1)
-        grads += [grad_out, grad_up, grad_down]
+        grads = [grad * factor for grad in (*grads, grad_out, grad_up, grad_down)]
         grad_input = (grad_first + contract_cols(grad_qkv, qkv_full)).astype(BF16)
         sums = jnp.concatenate(
             [
@@ -1298,14 +1328,14 @@
             ]
         )
         sums = lax.psum(sums, ("dp", "tensor")) * factor
-    v_out, v_down, v_gain_attn, v_shift_attn, v_gain_ffn, v_shift_ffn, v_query, v_value = (
-        sums[k * model_width : (k + 1) * model_width] for k in range(8)
-    )
-    v_up = sums[8 * model_width :]
+        vector_sums = jnp.split(sums, [k * model_width for k in range(1, 9)])
+    (
+        v_out, v_down, v_gain_attn, v_shift_attn, v_gain_ffn, v_shift_ffn, v_query, v_value, v_up,
+    ) = vector_sums
     return (
         output,
         grad_input,
-        *(grad * factor for grad in grads),
+        *grads,
         v_query,
         v_value,
         v_out,

time: 261 us -> 254 us (0.973)
  other arithmetic: 6.54 us -> 0 us
  local copies, waits for them, and re-layouts: 4.47 us -> 0 us
  Pallas kernels: 249 us -> 253 us
    mul x4 -> x0, other arithmetic: 6.54 us -> none  [the longest x3 5.65 us: layer(): grad * factor]
    pallas_call x0 -> x1, Pallas kernels: none -> 4.01 us  [scale_and_copy(): pl.pallas_call(body, out_shape=[jax.ShapeDtypeStruct(array.shape, array.d...]
    unnamed x4 -> x0, local copies, waits for them, and re-layouts: 3.24 us -> none
where the time goes in v1:
time: 254 us
  Pallas kernels  253 us (100%)
    pallas_call x1, Pallas kernels, forward_near(): pl.pallas_call(body, out_shape=[jax.ShapeDtypeStruct(shape, BF16) for sha...  127 us
    pallas_call x1, Pallas kernels, backward_near(): pl.pallas_call(body, out_shape=[jax.ShapeDtypeStruct((block, attn), F32)]...  122 us

profile of v1, /device:TPU:0, one launch (start us, length us, event | category | flops | bytes accessed | tf_op | source)
XLA Modules:
  0.0 253.9 jit_solution(589776207148226059)
XLA Ops:
  0.7 127.3 %forward_near.1 = (bf16[1024,3072]{1,0:T(8,128)(2,1)}, bf16[1024,1024]{1,0:T(8,128)(2,1)}, bf16[1024,4096]{1,0:T(8,128)(2,1)}, bf16[1024,4096]{1,0:T(8,128)(2,1)...) custom-call(f32[128,256]{1,0:T(8,128)} %q_in.1, ...), custom_call_target="tpu_custom_call" | custom-call | flops 12884901888 | bytes 50331648 | tf_op jit(solution)/shard_map/forward_near/pallas_call | solution.py:471
  127.9 121.8 %backward_near.1 = (f32[128,256]{1,0:T(8,128)}, f32[128,256]{1,0:T(8,128)}, f32[128,256]{1,0:T(8,128)}, f32[128,256]{1,0:T(8,128)}, f32[128,1024]{1,0:T(8,128)},...) custom-call(bf16[512,1024]{1,0:T(8,128)(2,1)} %get-tuple-element.59.mixed_in, ...), custom_call_target="tpu_custom_call" | custom-call | flops 25769803776 | bytes 50331648 | tf_op jit(solution)/shard_map/backward_near/pallas_call | solution.py:991
  249.7 4.0 %shard_map.305 = (f32[128,256]{1,0:T(8,128)}, f32[128,256]{1,0:T(8,128)}, f32[128,256]{1,0:T(8,128)}, f32[128,256]{1,0:T(8,128)}, f32[128,1024]{1,0:T(8,128)}, /...) custom-call(f32[128,256]{1,0:T(8,128)} %get-tuple-element.75.refs_0_, ...), custom_call_target="tpu_custom_call" | custom-call | tf_op jit(solution)/shard_map/pallas_call | solution.py:127

commit v2 on v1

--- a/solution.py
+++ b/solution.py
@@ -38,11 +38,12 @@
 TILE = 512
 
 FORWARD = (
-    "lplane9", "z1", "z3", "lcor9", "col1", "z2", "z5", "z0", "z4", "col3", "col2", "prep",
-    "col5", "col0", "cor2", "cor1", "z6", "cor0", "cor3", "z7", "last0", "z8", "col4", "col6",
-    "last2", "tr", "last1", "cor5", "cor4", "qkv", "last3", "lz9", "a0", "cor6", "a1", "a2",
-    "col7", "a3", "last4", "last5", "last6", "out", "col8", "norm", "up1", "cor7", "cor8",
-    "lcore9", "up2", "up3", "last7", "lowX", "last8", "low1", "low2", "ln",
+    "z3", "lplane9", "fw3", "lcor9", "z1", "col3", "fw1", "z6", "z0", "col1", "fw0", "cor3",
+    "z2", "col0", "fw2", "z5", "z4", "prep", "fw6", "z8", "cor1", "fw5", "last3", "col2", "fw4",
+    "cor0", "cor2", "tr", "fw8", "col5", "z7", "last1", "last0", "col4", "col6", "last2", "fw7",
+    "lz9", "qkv", "a0", "cor5", "cor4", "a1", "a2", "a3", "out", "fw9", "last5", "cor6", "col7",
+    "norm", "col8", "last4", "last6", "up1", "cor7", "up2", "lcore9", "cor8", "up3", "last7",
+    "lowX", "last8", "low1", "low2", "ln",
 )
 BACKWARD = (
     "oth8", "oth7", "gelA", "own8", "cor8", "own7", "cor7", "oth9", "oth4", "sid8", "gelB",
@@ -144,6 +145,7 @@
     half = block // 2
     pieces = pieces_of(size, attn, units_each)
     X = len(pieces) - 1
+    pieces = pieces[:-3] + [pieces[-2], pieces[-1], pieces[-3]]
     A, O, U, _ = range(4)
     B_OUT, B_DOWN, G_ATTN, S_ATTN, G_FFN, S_FFN = range(6)
 
@@ -170,20 +172,28 @@
         by_x, by_y, by_core = dp_partner(BIT_X), dp_partner(BIT_Y), dp_partner(BIT_CORE)
         owners = [block_of(data_at, mask) for mask in ORDER]
         copies = {}
-
-        def send(g, slot, source, target, device):
+        sent = {}
+
+        def send(g, slot, source, target, device, when=None, lands=None):
             def copy():
                 return pltpu.make_async_remote_copy(
                     src_ref=source,
                     dst_ref=target,
                     send_sem=send_sem.at[g, slot],
-                    recv_sem=recv_sem.at[g, slot],
+                    recv_sem=recv_sem.at[g, slot if lands is None else lands],
                     device_id=device,
                     device_id_type=pl.DeviceIdType.MESH,
                 )
 
             copies[g, slot] = copy
-            copy().start()
+            only(when, lambda: copy().start())
+            sent[g, slot] = when
+
+        def only(when, step):
+            if when is None:
+                step()
+            else:
+                pl.when(when())(step)
 
         def arrived(g, *slots):
             for slot in slots:
@@ -198,12 +208,18 @@
             at = first + r * wide_by
             return places[weight].at[start : start + count, at : at + wide_by]
 
-        def send_z(g):
-            for r in range(1, size):
-                send(g, r - 1, cell(g, 0, block, 0), cell(g, 0, block, r), z_partner(r))
+        def send_z(g, count=block):
+            send(g, 1, cell(g, 0, count, 0), cell(g, 0, count, 2), z_partner(2))
+            send(g, 0, cell(g, 0, count, 0), cell(g, 0, count, 1), z_partner(1), lambda: tensor_at < size - 1)
+            send(g, 2, cell(g, 0, count, 0), cell(g, 0, count, 3), z_partner(3), lambda: tensor_at > 0)
+
+        def pass_on(g, count=block):
+            arrived(g, 1)
+            send(g, 9, cell(g, 0, count, 2), cell(g, 0, count, 1), z_partner(3), lambda: tensor_at == 1, 0)
+            send(g, 10, cell(g, 0, count, 2), cell(g, 0, count, 3), z_partner(1), lambda: tensor_at == 2, 2)
 
         def send_column(g):
-            arrived(g, 0, 1, 2)
+            arrived(g, 0, 2)
             send(g, 3, whole(g, 0, block), whole(g, block, block), by_x)
             send(g, 4, whole(g, 0, block), whole(g, 2 * block, block), by_y)
 
@@ -232,11 +248,10 @@
 
         def late_z():
             arrived(X, 5, 6)
-            for r in range(1, size):
-                send(X, r - 1, cell(X, 0, 4 * block, 0), cell(X, 0, 4 * block, r), z_partner(r))
+            send_z(X, 4 * block)
 
         def late_core():
-            arrived(X, 0, 1, 2)
+            arrived(X, 0, 2)
             send(X, 7, whole(X, 0, 4 * block), whole(X, 4 * block, 4 * block), by_core)
 
         saves = []
@@ -444,10 +459,11 @@
             "prep": prepare, "tr": turn_inputs, "qkv": qkv, "out": out, "norm": norm, "ln": last_norm,
             "up1": bound(raise_piece, 4), "up2": bound(raise_piece, 5), "up3": bound(raise_piece, 6),
             "low1": bound(lower_piece, 7), "low2": bound(lower_piece, 8), "lowX": bound(lower_piece, X),
-            "lplane9": late_plane, "lcor9": late_corner, "lz9": late_z, "lcore9": late_core,
+            "fw9": bound(pass_on, X, 4 * block), "lplane9": late_plane, "lcor9": late_corner, "lz9": late_z, "lcore9": late_core,
         }
         for g in range(X):
             table[f"z{g}"] = bound(send_z, g)
+            table[f"fw{g}"] = bound(pass_on, g)
             table[f"col{g}"] = bound(send_column, g)
             table[f"cor{g}"] = bound(send_corner, g)
             table[f"last{g}"] = bound(send_last, g)
@@ -462,8 +478,8 @@
             slope_copy(j).wait()
         for copy in saves:
             copy.wait()
-        for copy in copies.values():
-            copy().wait_send()
+        for key, copy in copies.items():
+            only(sent[key], lambda: copy().wait_send())
 
     anywhere, inside = pl.BlockSpec(memory_space=pl.ANY), pl.BlockSpec(memory_space=pltpu.VMEM)
     tall = jax.ShapeDtypeStruct((rows, width), BF16)
@@ -502,8 +518,8 @@
             pltpu.VMEM((width, rows), BF16),
             pltpu.VMEM((width, rows), BF16),
             pltpu.SemaphoreType.DMA((5 + len(pieces),)),
-            pltpu.SemaphoreType.DMA((len(pieces), 9)),
-            pltpu.SemaphoreType.DMA((len(pieces), 9)),
+            pltpu.SemaphoreType.DMA((len(pieces), 11)),
+            pltpu.SemaphoreType.DMA((len(pieces), 11)),
             pltpu.SemaphoreType.DMA((2, units // TILE)),
         ],
         compiler_params=pltpu.CompilerParams(
@@ -1240,7 +1256,7 @@
     matrices = (w_query, w_key, w_value, w_out, w_up, w_down)
     wide = (bias_out, bias_down, gain_attn, shift_attn, gain_ffn, shift_ffn)
 
-    if n_data == len(ORDER) and spread_over == 1:
+    if n_data == len(ORDER) and n_tensor == 4 and spread_over == 1:
         (
             qkv_full, out_full, up_full, down_full, qkv, context, hidden, active, slope, output,
             mixed_low, mixed_t, normed_t, input_t, grad_second, given, arranged,

time: 254 us -> 239 us (0.941)
  Pallas kernels: 253 us -> 238 us
    pallas_call x1, Pallas kernels: 127 us -> 113 us  [forward_near(): pl.pallas_call(body, out_shape=[jax.ShapeDtypeStruct(shape, BF16) for sha...]
where the time goes in v2:
time: 239 us
  Pallas kernels  238 us (100%)
    pallas_call x1, Pallas kernels, backward_near(): pl.pallas_call(body, out_shape=[jax.ShapeDtypeStruct((block, attn), F32)]...  121 us
    pallas_call x1, Pallas kernels, forward_near(): pl.pallas_call(body, out_shape=[jax.ShapeDtypeStruct(shape, BF16) for sha...  113 us

profile of v2, /device:TPU:0, one launch (start us, length us, event | category | flops | bytes accessed | tf_op | source)
XLA Modules:
  0.0 238.7 jit_solution(7924090710412827445)
XLA Ops:
  0.7 112.8 %forward_near.1 = (bf16[1024,3072]{1,0:T(8,128)(2,1)}, bf16[1024,1024]{1,0:T(8,128)(2,1)}, bf16[1024,4096]{1,0:T(8,128)(2,1)}, bf16[1024,4096]{1,0:T(8,128)(2,1)...) custom-call(f32[128,256]{1,0:T(8,128)} %q_in.1, ...), custom_call_target="tpu_custom_call" | custom-call | flops 12884901888 | bytes 50331648 | tf_op jit(solution)/shard_map/forward_near/pallas_call | solution.py:487
  113.5 121.1 %backward_near.1 = (f32[128,256]{1,0:T(8,128)}, f32[128,256]{1,0:T(8,128)}, f32[128,256]{1,0:T(8,128)}, f32[128,256]{1,0:T(8,128)}, f32[128,1024]{1,0:T(8,128)},...) custom-call(bf16[512,1024]{1,0:T(8,128)(2,1)} %get-tuple-element.59.mixed_in, ...), custom_call_target="tpu_custom_call" | custom-call | flops 25769803776 | bytes 50331648 | tf_op jit(solution)/shard_map/backward_near/pallas_call | solution.py:1007
  234.5 4.0 %shard_map.305 = (f32[128,256]{1,0:T(8,128)}, f32[128,256]{1,0:T(8,128)}, f32[128,256]{1,0:T(8,128)}, f32[128,256]{1,0:T(8,128)}, f32[128,1024]{1,0:T(8,128)}, /...) custom-call(f32[128,256]{1,0:T(8,128)} %get-tuple-element.75.refs_0_, ...), custom_call_target="tpu_custom_call" | custom-call | tf_op jit(solution)/shard_map/pallas_call | solution.py:128

commit v3 on v2

--- a/solution.py
+++ b/solution.py
@@ -38,21 +38,22 @@
 TILE = 512
 
 FORWARD = (
-    "z3", "lplane9", "fw3", "lcor9", "z1", "col3", "fw1", "z6", "z0", "col1", "fw0", "cor3",
-    "z2", "col0", "fw2", "z5", "z4", "prep", "fw6", "z8", "cor1", "fw5", "last3", "col2", "fw4",
-    "cor0", "cor2", "tr", "fw8", "col5", "z7", "last1", "last0", "col4", "col6", "last2", "fw7",
-    "lz9", "qkv", "a0", "cor5", "cor4", "a1", "a2", "a3", "out", "fw9", "last5", "cor6", "col7",
-    "norm", "col8", "last4", "last6", "up1", "cor7", "up2", "lcore9", "cor8", "up3", "last7",
-    "lowX", "last8", "low1", "low2", "ln",
+    "lplane9", "z3", "fw3", "z1", "lcor9", "col3", "fw1", "z2", "fw2", "col1", "z0", "col2",
+    "cor3", "z8", "z6", "fw0", "cor1", "z4", "z7", "z5", "col0", "cor2", "fw6", "prep", "fw8",
+    "cor0", "tr", "col6", "fw4", "fw5", "lz9", "col4", "last2", "last0", "last1", "qkv", "a0",
+    "cor6", "col5", "a1", "a2", "fw7", "last3", "a3", "out", "cor4", "fw9", "norm", "cor5",
+    "last4", "col7", "col8", "last5", "last6", "up1", "lcore9", "up2", "cor7", "up3", "cor8",
+    "lowX", "last7", "last8", "low1", "low2", "ln",
 )
 BACKWARD = (
-    "oth8", "oth7", "gelA", "own8", "cor8", "own7", "cor7", "oth9", "oth4", "sid8", "gelB",
-    "own9", "sid7", "oth5", "lz9", "oth6", "upA", "own4", "upB", "own5", "cor4", "cor5", "norm",
-    "col8", "sid4", "own6", "out", "col7", "oth3", "a0", "own3", "cor3", "cor6", "a1", "col4",
-    "sid5", "sid3", "a2", "a3", "oth1", "sid6", "vec", "oth2", "col5", "fin4", "own1", "cor1",
-    "v0", "oth0", "col3", "v1", "own2", "cor2", "fin8", "sid1", "col6", "own0", "cor0", "fin7",
-    "sid2", "v2", "col1", "dxA", "sid0", "col2", "lcor9", "dxB", "fin6", "col0", "v3", "sid9",
-    "fin2", "v4", "gout", "fin5", "fin1", "fin3", "fin9", "v5", "fin0",
+    "oth7", "oth9", "gelA", "own7", "oth8", "cor7", "oth4", "gelB", "own9", "own8", "cor8",
+    "lz9", "own4", "cor4", "sid7", "upA", "upB", "oth5", "oth6", "sid4", "sid8", "norm", "out",
+    "own5", "own6", "cor5", "a0", "col4", "col7", "cor6", "oth3", "a1", "sid5", "own3", "cor3",
+    "fw9", "sid6", "a2", "a3", "oth2", "fw4", "sid3", "oth0", "vec", "oth1", "col8", "own2",
+    "own0", "cor0", "col5", "own1", "col6", "v0", "cor2", "fw8", "fw7", "cor1", "fin4", "fw5",
+    "sid0", "dxA", "fw6", "col3", "sid1", "fin7", "v1", "dxB", "sid2", "fw3", "col0", "v2",
+    "col1", "fw0", "lcor9", "gout", "col2", "fin6", "fin8", "fin5", "v3", "sid9", "fw1", "fin0",
+    "fin3", "fw2", "v4", "fin9", "fin1", "fin2", "v5",
 )
 
 
@@ -550,6 +551,7 @@
     attn = full[1] // size
     pieces = pieces_of(size, attn, units_each)
     X = len(pieces) - 1
+    pieces = pieces[:-3] + [pieces[-2], pieces[-1], pieces[-3]]
     A, O, U, D = range(4)
     tiles = [c // TILE for c in full]
     vector_rows = (6 * width + 2 * full[1] + units) // 128
@@ -564,10 +566,10 @@
         units_sum, mixed_ref, normed_t, input_t, context_ref, a_plane, o_plane, u_plane, d_plane, *rest,
     ):
         count = len(pieces)
-        corners, sides, zins = (rest[k * count : (k + 1) * count] for k in range(3))
+        corners, sides, zins, relays = (rest[k * count : (k + 1) * count] for k in range(4))
         (
             v_ref, v_in, load_sem, start_sem, core_send, core_recv, send_sem, recv_sem, v_send, v_recv,
-        ) = rest[3 * count :]
+        ) = rest[4 * count :]
         data_at, tensor_at = lax.axis_index("dp"), lax.axis_index("tensor")
         planes = (a_plane, o_plane, u_plane, d_plane)
         outs = (q_out, k_out, v_out, o_out, u_out, u_out, u_out, d_out, d_out, d_out)
@@ -628,13 +630,70 @@
             )
 
         copies = {}
-
-        def send(g, slot, source, target, device):
+        sent = {}
+
+        def send(g, slot, source, target, device, when=None, lands=None):
             def copy():
-                return remote(source, target(), send_sem.at[g, slot], recv_sem.at[g, slot], device)
+                at = slot if lands is None else lands
+                return remote(source, target(), send_sem.at[g, slot], recv_sem.at[g, at], device)
 
             copies[g, slot] = copy
-            copy().start()
+            sent[g, slot] = when
+            only(when, lambda: copy().start())
+
+        def only(when, step):
+            if when is None:
+                step()
+            else:
+                pl.when(when())(step)
+
+        def not_first():
+            return tensor_at > 0
+
+        def not_last():
+            return tensor_at < size - 1
+
+        def first_one():
+            return tensor_at == 0
+
+        def last_one():
+            return tensor_at == size - 1
+
+        def outer():
+            return (tensor_at % (size - 1)) == 0
+
+        def inner():
+            return (tensor_at % (size - 1)) > 0
+
+        def z_cell(g, r, count):
+            weight, first, wide_by = pieces[g]
+            at = first + r * wide_by
+            return planes[weight].at[:count, at : at + wide_by]
+
+        def send_z(g, count=block):
+            near, far = z_cell(g, 1, count), z_cell(g, 3, count)
+            send(g, 7, near, lambda: relays[g], z_partner(1), first_one)
+            send(g, 8, far, lambda: relays[g], z_partner(-1), last_one, 7)
+            send(g, 4, near, lambda: zins[g].at[0], z_partner(-1), not_first)
+            send(g, 6, far, lambda: zins[g].at[2], z_partner(1), not_last)
+            send(g, 5, z_cell(g, 2, count), lambda: zins[g].at[1], z_partner(-2), outer)
+
+        def add_on(g, count=block):
+            def step():
+                arrived(g, 7)
+                cell = z_cell(g, 2, count)
+                for at in range(0, count, block):
+                    rows_k = slice(at, at + block)
+                    total = cell[rows_k, :].astype(F32) + relays[g][rows_k, :].astype(F32)
+                    cell[rows_k, :] = total.astype(BF16)
+
+            only(inner, step)
+            send(g, 9, z_cell(g, 2, count), lambda: zins[g].at[1], z_partner(-2), inner, 5)
+
+        def wait_z(g):
+            arrived(g, 5)
+            only(not_last, lambda: arrived(g, 4))
+            only(not_first, lambda: arrived(g, 6))
 
         def arrived(g, *slots):
             for slot in slots:
@@ -696,26 +755,29 @@
                     out_of(g)[...] = total
                 else:
                     planes[weight][:block, own] = total.astype(BF16)
-                    send(g, 3 + r, planes[weight].at[:block, own], lambda r=r: zins[g].at[r - 1], z_partner(-r))
+            send_z(g)
 
         def finish(g):
-            arrived(g, *range(4, 3 + size))
-            total = out_of(g)[...]
-            for r in range(1, size):
-                total += zins[g][r - 1].astype(F32)
-            out_of(g)[...] = total
-
-        def late_z():
-            weight, first, wide_by = pieces[X]
-            for r in range(1, size):
-                own = slice(first + r * wide_by, first + (r + 1) * wide_by)
-                send(X, 3 + r, planes[weight].at[:, own], lambda r=r: zins[X].at[r - 1], z_partner(-r))
+            wait_z(g)
+
+            def add(k):
+                out_of(g)[...] += zins[g][k].astype(F32)
+
+            add(1)
+            only(not_last, lambda: add(0))
+            only(not_first, lambda: add(2))
 
         def late_corner():
-            arrived(X, *range(4, 3 + size))
-            for k in range(4):
-                rows_k = slice(k * block, (k + 1) * block)
-                add_rows(X, k * block, block, *(zins[X].at[r, rows_k] for r in range(size - 1)))
+            wait_z(X)
+
+            def add(z):
+                for k in range(4):
+                    rows_k = slice(k * block, (k + 1) * block)
+                    add_rows(X, k * block, block, zins[X].at[z, rows_k])
+
+            add(1)
+            only(not_last, lambda: add(0))
+            only(not_first, lambda: add(2))
             send_corner(X)
 
         def late_finish():
@@ -968,7 +1030,8 @@
             "dxA": bound(over_tiles, 0, halves[A][1], weight_loads[A], input_step),
             "dxB": bound(over_tiles, *halves[A][1:], weight_loads[A], input_step),
             "gout": give_input,
-            "lz9": late_z,
+            "lz9": bound(send_z, X, 4 * block),
+            "fw9": bound(add_on, X, 4 * block),
             "lcor9": late_corner,
             "sid9": bound(send_sides, X),
             "fin9": late_finish,
@@ -986,6 +1049,7 @@
                 table[f"sid{g}"] = bound(send_sides, g)
                 table[f"col{g}"] = bound(send_column, g)
                 table[f"fin{g}"] = bound(finish, g)
+                table[f"fw{g}"] = bound(add_on, g)
         table["oth3"] = lambda: None
         table["own3"] = own_out
         first_up = [g for g in range(len(pieces)) if f"oth{g}" in BACKWARD and pieces[g][0] == U]
@@ -999,8 +1063,8 @@
                 core_copy(g, j).wait_send()
         for k in range(5):
             v_copy(k).wait_send()
-        for copy in copies.values():
-            copy().wait_send()
+        for key, copy in copies.items():
+            only(sent[key], lambda: copy().wait_send())
 
     spans = [piece[2] if g == X else size * piece[2] for g, piece in enumerate(pieces)]
     anywhere, inside = pl.BlockSpec(memory_space=pl.ANY), pl.BlockSpec(memory_space=pltpu.VMEM)
@@ -1043,14 +1107,18 @@
             for g, piece in enumerate(pieces)
         ]
         + [
+            pltpu.VMEM((4 * block if g == X else block, piece[2]), BF16)
+            for g, piece in enumerate(pieces)
+        ]
+        + [
             pltpu.VMEM((6, vector_rows, 128), F32),
             pltpu.VMEM((5, vector_rows, 128), F32),
             pltpu.SemaphoreType.DMA((3, 2)),
             pltpu.SemaphoreType.DMA((7,)),
             pltpu.SemaphoreType.DMA((4, units // TILE)),
             pltpu.SemaphoreType.DMA((4, units // TILE)),
-            pltpu.SemaphoreType.DMA((len(pieces), 3 + size)),
-            pltpu.SemaphoreType.DMA((len(pieces), 3 + size)),
+            pltpu.SemaphoreType.DMA((len(pieces), 10)),
+            pltpu.SemaphoreType.DMA((len(pieces), 10)),
             pltpu.SemaphoreType.DMA((5,)),
             pltpu.SemaphoreType.DMA((5,)),
         ],

time: 239 us -> 243 us (1.017)
  Pallas kernels: 238 us -> 242 us
    pallas_call x1, Pallas kernels: 121 us -> 126 us  [backward_near(): pl.pallas_call(body, out_shape=[jax.ShapeDtypeStruct((block, attn), F32)]...]
where the time goes in v3:
time: 243 us; the launch traced here: 242 us
  Pallas kernels  242 us (100%)
    pallas_call x1, Pallas kernels, backward_near(): pl.pallas_call(body, out_shape=[jax.ShapeDtypeStruct((block, attn), F32)]...  126 us
    pallas_call x1, Pallas kernels, forward_near(): pl.pallas_call(body, out_shape=[jax.ShapeDtypeStruct(shape, BF16) for sha...  112 us

profile of v3, /device:TPU:0, one launch (start us, length us, event | category | flops | bytes accessed | tf_op | source)
XLA Modules:
  0.0 242.4 jit_solution(2458307685738346380)
XLA Ops:
  0.7 112.0 %forward_near.1 = (bf16[1024,3072]{1,0:T(8,128)(2,1)}, bf16[1024,1024]{1,0:T(8,128)(2,1)}, bf16[1024,4096]{1,0:T(8,128)(2,1)}, bf16[1024,4096]{1,0:T(8,128)(2,1)...) custom-call(f32[128,256]{1,0:T(8,128)} %q_in.1, ...), custom_call_target="tpu_custom_call" | custom-call | flops 12884901888 | bytes 50331648 | tf_op jit(solution)/shard_map/forward_near/pallas_call | solution.py:488
  112.7 125.6 %backward_near.1 = (f32[128,256]{1,0:T(8,128)}, f32[128,256]{1,0:T(8,128)}, f32[128,256]{1,0:T(8,128)}, f32[128,256]{1,0:T(8,128)}, f32[128,1024]{1,0:T(8,128)},...) custom-call(bf16[512,1024]{1,0:T(8,128)(2,1)} %get-tuple-element.59.mixed_in, ...), custom_call_target="tpu_custom_call" | custom-call | flops 25769803776 | bytes 50331648 | tf_op jit(solution)/shard_map/backward_near/pallas_call | solution.py:1071
  238.2 4.0 %shard_map.305 = (f32[128,256]{1,0:T(8,128)}, f32[128,256]{1,0:T(8,128)}, f32[128,256]{1,0:T(8,128)}, f32[128,256]{1,0:T(8,128)}, f32[128,1024]{1,0:T(8,128)}, /...) custom-call(f32[128,256]{1,0:T(8,128)} %get-tuple-element.75.refs_0_, ...), custom_call_target="tpu_custom_call" | custom-call | tf_op jit(solution)/shard_map/pallas_call | solution.py:129

commit v4 on v2

--- a/solution.py
+++ b/solution.py
@@ -38,12 +38,12 @@
 TILE = 512
 
 FORWARD = (
-    "z3", "lplane9", "fw3", "lcor9", "z1", "col3", "fw1", "z6", "z0", "col1", "fw0", "cor3",
-    "z2", "col0", "fw2", "z5", "z4", "prep", "fw6", "z8", "cor1", "fw5", "last3", "col2", "fw4",
-    "cor0", "cor2", "tr", "fw8", "col5", "z7", "last1", "last0", "col4", "col6", "last2", "fw7",
-    "lz9", "qkv", "a0", "cor5", "cor4", "a1", "a2", "a3", "out", "fw9", "last5", "cor6", "col7",
-    "norm", "col8", "last4", "last6", "up1", "cor7", "up2", "lcore9", "cor8", "up3", "last7",
-    "lowX", "last8", "low1", "low2", "ln",
+    "lplane9", "z3", "fw3", "z1", "lcor9", "col3", "fw1", "z2", "fw2", "col1", "z0", "col2",
+    "cor3", "z8", "z6", "fw0", "cor1", "z4", "z7", "z5", "col0", "cor2", "fw6", "prep", "fw8",
+    "cor0", "tr", "col6", "fw4", "fw5", "lz9", "col4", "last2", "last0", "last1", "qkv", "a0",
+    "cor6", "col5", "a1", "a2", "fw7", "last3", "a3", "out", "cor4", "fw9", "norm", "cor5",
+    "last4", "col7", "col8", "last5", "last6", "up1", "lcore9", "up2", "cor7", "up3", "cor8",
+    "lowX", "last7", "last8", "low1", "low2", "ln",
 )
 BACKWARD = (
     "oth8", "oth7", "gelA", "own8", "cor8", "own7", "cor7", "oth9", "oth4", "sid8", "gelB",

time: 239 us -> 243 us (1.017)
  Pallas kernels: 238 us -> 242 us
    pallas_call x1, Pallas kernels: 121 us -> 126 us  [backward_near(): pl.pallas_call(body, out_shape=[jax.ShapeDtypeStruct((block, attn), F32)]...]
where the time goes in v4:
time: 243 us; the launch traced here: 242 us
  Pallas kernels  242 us (100%)
    pallas_call x1, Pallas kernels, backward_near(): pl.pallas_call(body, out_shape=[jax.ShapeDtypeStruct((block, attn), F32)]...  126 us
    pallas_call x1, Pallas kernels, forward_near(): pl.pallas_call(body, out_shape=[jax.ShapeDtypeStruct(shape, BF16) for sha...  112 us

profile of v4, /device:TPU:0, one launch (start us, length us, event | category | flops | bytes accessed | tf_op | source)
XLA Modules:
  0.0 242.3 jit_solution(16985528664959513578)
XLA Ops:
  0.7 112.0 %forward_near.1 = (bf16[1024,3072]{1,0:T(8,128)(2,1)}, bf16[1024,1024]{1,0:T(8,128)(2,1)}, bf16[1024,4096]{1,0:T(8,128)(2,1)}, bf16[1024,4096]{1,0:T(8,128)(2,1)...) custom-call(f32[128,256]{1,0:T(8,128)} %q_in.1, ...), custom_call_target="tpu_custom_call" | custom-call | flops 12884901888 | bytes 50331648 | tf_op jit(solution)/shard_map/forward_near/pallas_call | solution.py:487
  112.7 125.5 %backward_near.1 = (f32[128,256]{1,0:T(8,128)}, f32[128,256]{1,0:T(8,128)}, f32[128,256]{1,0:T(8,128)}, f32[128,256]{1,0:T(8,128)}, f32[128,1024]{1,0:T(8,128)},...) custom-call(bf16[512,1024]{1,0:T(8,128)(2,1)} %get-tuple-element.59.mixed_in, ...), custom_call_target="tpu_custom_call" | custom-call | flops 25769803776 | bytes 50331648 | tf_op jit(solution)/shard_map/backward_near/pallas_call | solution.py:1007
  238.2 4.0 %shard_map.305 = (f32[128,256]{1,0:T(8,128)}, f32[128,256]{1,0:T(8,128)}, f32[128,256]{1,0:T(8,128)}, f32[128,256]{1,0:T(8,128)}, f32[128,1024]{1,0:T(8,128)}, /...) custom-call(f32[128,256]{1,0:T(8,128)} %get-tuple-element.75.refs_0_, ...), custom_call_target="tpu_custom_call" | custom-call | tf_op jit(solution)/shard_map/pallas_call | solution.py:128
